TPU v7x, 32 devices: a whole 2x2x4 slice. The times are simulated.
32 devices in a mesh: row: 4 (over y, x), col: 8 (over z, core).
Axes of the slice: x: 2, y: 2, z: 4, core: 2. Of those that a mesh axis runs over, the one named last changes fastest.
Arguments:
- mlp_param: float32 [6144, 24576], P('row', 'col'), may hold values from -250 to 250
- mlp_grad: bfloat16 [6144, 24576], P('row', 'col'), may hold values from -250 to 250
- mlp_row_state: float32 [6144], P('row'), may hold values from 0.03 to 2.7
- mlp_col_state: float32 [24576], P('col'), may hold values from 0.02 to 0.3
- attn_param: float32 [6144, 6144], P('row', 'col'), may hold values from -250 to 250
- attn_grad: bfloat16 [6144, 6144], P('row', 'col'), may hold values from -250 to 250
- attn_row_state: float32 [6144], P('row'), may hold values from 0.03 to 2.7
- attn_col_state: float32 [6144], P('col'), may hold values from 0.02 to 0.3
Outputs:
- mlp_param_new: float32 [6144, 24576], P('row', 'col')
- attn_param_new: float32 [6144, 6144], P('row', 'col')
- mlp_row_new: float32 [6144], P('row')
- mlp_col_new: float32 [24576], P('col')
- attn_row_new: float32 [6144], P('row')
- attn_col_new: float32 [6144], P('col')
- attn_copy: bfloat16 [6144, 6144], P(None, 'col')
All inputs are finite; a program needn't handle non-finite values.
Results may differ from a plain program's by a relative error of at most 0.0004.
Values may be sent and summed in bfloat16 or wider, within the bound.
A program may use at most 128 MiB of HBM per device.

v0:
```python
import jax
import jax.numpy as jnp
from jax import lax
from jax.sharding import PartitionSpec as P

STEP = 4
TINY_SQUARE = 1e-30
LEARN_RATE = 0.05
DECAY_POWER = 0.8


def local(
    mlp_param,
    mlp_grad,
    mlp_row_state,
    mlp_col_state,
    attn_param,
    attn_grad,
    attn_row_state,
    attn_col_state,
):
    keep_rate = 1.0 - STEP ** (-DECAY_POWER)
    block_rows = mlp_grad.shape[0]
    rows_total = block_rows * lax.axis_size("row")
    mlp_width = mlp_grad.shape[1] * lax.axis_size("col")
    attn_width = attn_grad.shape[1] * lax.axis_size("col")
    mlp_count = float(rows_total * mlp_width)
    attn_count = float(rows_total * attn_width)
    mlp_square = jnp.square(mlp_grad.astype(jnp.float32)) + TINY_SQUARE
    attn_square = jnp.square(attn_grad.astype(jnp.float32)) + TINY_SQUARE
    param_local = (jnp.sum(jnp.square(mlp_param)), jnp.sum(jnp.square(attn_param)))
    param_mlp, param_attn = lax.psum((param_local[0], param_local[1]), ("row", "col"))
    row_mlp, row_attn = lax.psum((jnp.sum(mlp_square, axis=1), jnp.sum(attn_square, axis=1)), "col")
    mlp_rows_new = keep_rate * mlp_row_state + (1.0 - keep_rate) * (row_mlp / mlp_width)
    attn_rows_new = keep_rate * attn_row_state + (1.0 - keep_rate) * (row_attn / attn_width)
    col_mlp, col_attn = lax.psum((jnp.sum(mlp_square, axis=0), jnp.sum(attn_square, axis=0)), "row")
    mlp_cols_new = keep_rate * mlp_col_state + (1.0 - keep_rate) * (col_mlp / rows_total)
    attn_cols_new = keep_rate * attn_col_state + (1.0 - keep_rate) * (col_attn / rows_total)
    mlp_raw = mlp_grad.astype(jnp.float32) / jnp.sqrt(mlp_rows_new[:, None] * mlp_cols_new[None, :])
    attn_raw = attn_grad.astype(jnp.float32) / jnp.sqrt(
        attn_rows_new[:, None] * attn_cols_new[None, :]
    )
    clip_local = (jnp.sum(jnp.square(mlp_raw)), jnp.sum(jnp.square(attn_raw)))
    clip_mlp, clip_attn = lax.psum((clip_local[0], clip_local[1]), ("row", "col"))
    mlp_clip = jnp.maximum(1.0, jnp.sqrt(clip_mlp / mlp_count))
    attn_clip = jnp.maximum(1.0, jnp.sqrt(clip_attn / attn_count))
    mlp_step = LEARN_RATE * jnp.sqrt(param_mlp / mlp_count)
    attn_step = LEARN_RATE * jnp.sqrt(param_attn / attn_count)
    mlp_new = mlp_param - mlp_step * (mlp_raw / mlp_clip)
    attn_new = attn_param - attn_step * (attn_raw / attn_clip)
    weight_copy = lax.all_gather(attn_new.astype(jnp.bfloat16), "row", axis=0, tiled=True)
    return (
        mlp_new,
        attn_new,
        mlp_rows_new,
        mlp_cols_new,
        attn_rows_new,
        attn_cols_new,
        weight_copy,
    )


def solution(mesh):
    return jax.shard_map(
        local,
        mesh=mesh,
        in_specs=(
            P("row", "col"),
            P("row", "col"),
            P("row"),
            P("col"),
            P("row", "col"),
            P("row", "col"),
            P("row"),
            P("col"),
        ),
        out_specs=(
            P("row", "col"),
            P("row", "col"),
            P("row"),
            P("col"),
            P("row"),
            P("col"),
            P(None, "col"),
        ),
        check_vma=False,
    )
```

profile of v0, /device:TPU:0, one launch (start us, length us, event | category | flops | bytes accessed | tf_op | source)
XLA Modules:
  0.0 249.6 jit_solution(1990881381430585324)
XLA Ops:
  7.2 0.0 all-gather.2.cloned.1.call-start
  7.2 12.0 %multiply_reduce_fusion.1 = f32[]{:T(128)} fusion(f32[1536,3072]{1,0:T(8,128)} %param.8), kind=kLoop, calls=%fused_computation.7 | loop fusion | flops 9437183 | bytes 18874372 | tf_op jit(solution)/shard_map/reduce_sum | solution.py:31
  19.2 1.0 fusion.5
  20.2 0.0 copy-start.8
  20.2 0.0 slice-start
  20.2 13.0 %fusion.2 = (f32[1536]{0:T(1024)S(1)}, f32[3072]{0:T(1024)S(1)}) fusion(bf16[1536,3072]{1,0:T(8,128)(2,1)} %param.9), kind=kLoop, calls=%fused_computation.4 | loop fusion | flops 23588352 | bytes 9455616 | tf_op jit(solution)/shard_map/reduce_sum | solution.py:33
  33.2 30.3 %all-reduce.1 = (f32[1536]{0:T(1024)S(1)}, f32[1536]{0:T(1024)S(1)}) all-reduce(f32[1536]{0:T(1024)S(1)} %get-tuple-element.7, f32[1536]{0:T(1024)S(1)} %get-tuple-element.9), channel_id=1, replica_groups=mesh['row'=4,'col'=8] {'col'}, use_global_device_ids=true, to_apply=%region_3.0 | all-reduce | flops 3072 | bytes 24576 | tf_op jit(solution)/shard_map/psum | solution.py:33
  63.5 16.0 %all-reduce.2 = (f32[3072]{0:T(1024)S(1)}, f32[768]{0:T(1024)S(1)}) all-reduce(f32[3072]{0:T(1024)S(1)} %get-tuple-element.8, f32[768]{0:T(1024)S(1)} %get-tuple-element.10), channel_id=1, replica_groups=mesh['row'=4,'col'=8] {'row'}, use_global_device_ids=true, to_apply=%region_5.0 | all-reduce | flops 3840 | bytes 30720 | tf_op jit(solution)/shard_map/psum | solution.py:36
  79.6 0.0 copy-done.5
  79.6 0.0 copy-start.1
  79.6 0.0 copy-start.2
  79.6 0.0 copy-start.3
  79.7 0.0 slice-start.1
  79.7 9.5 %multiply_reduce_fusion = f32[]{:T(128)} fusion(bf16[1536,3072]{1,0:T(8,128)(2,1)} %param.9, f32[3072]{0:T(1024)S(1)} %multiply_add_fusion, f32[1536]{0:T(1024)S(1)} %get-tuple-element.32), kind=kLoop, calls=%fused_computation.6 | loop fusion | flops 23592960 | bytes 9455620 | tf_op jit(solution)/shard_map/reduce_sum | solution.py:43
  89.2 2.5 %multiply_reduce_fusion.2 = f32[]{:T(128)} fusion(bf16[1536,768]{1,0:T(8,128)(2,1)S(1)} %copy-done, f32[768]{0:T(1024)S(1)} %multiply_add_fusion.3, f32[1536]{0:T(1024)S(1)} %get-tuple-element.34), kind=kLoop, calls=%fused_computation.14 | loop fusion | flops 5898239 | bytes 2368516 | tf_op jit(solution)/shard_map/reduce_sum | solution.py:43
  91.7 1.9 multiply_reduce_fusion.3
  93.6 37.2 %all-reduce = (f32[]{:T(128)}, f32[]{:T(128)}, f32[]{:T(128)}, f32[]{:T(128)}) all-reduce(f32[]{:T(128)} %multiply_reduce_fusion, f32[]{:T(128)} %multiply_reduce_fusion.1, f32[]{:T(128)} %multiply_reduce_fusion.2, f32[]{:T(128)} %multiply_reduce_fusion.3), channel_id=1, replica_groups=mesh['row'=4,'col'=8] {'row','col'}, use_global_device_ids=true, to_apply=%region_7.0 | all-reduce | flops 4 | bytes 32 | tf_op jit(solution)/shard_map/psum | solution.py:44
  132.3 5.4 %fusion.6 = (bf16[1536,768]{1,0:T(8,128)(2,1)}, f32[1536,768]{1,0:T(8,128)}) fusion(f32[1536,768]{1,0:T(8,128)} %param.12, f32[]{:T(128)S(6)} %max.7, f32[768]{0:T(1024)S(1)} %multiply_add_fusion.3, f32[1536]{0:T(1024)S(1)} %get-tuple-element.34, bf16[1536,768]{1,0:T(8,128)(2,1)S(1)} %copy-done, f32[]{:T(128)S(6)} %mul.97), kind=kLoop, calls=%fused_computation.20 | loop fusion | flops 8257536 | bytes 14165000 | tf_op jit(solution)/shard_map/convert_element_type | solution.py:51
  137.7 0.0 all-gather.2.cloned.1.call-update
  139.1 0.0 copy-done.1
  139.1 0.0 copy-done.3
  139.1 19.4 %multiply_subtract_fusion = f32[1536,3072]{1,0:T(8,128)} fusion(f32[1536,3072]{1,0:T(8,128)} %param.8, bf16[1536,3072]{1,0:T(8,128)(2,1)} %param.9, f32[]{:T(128)S(6)} %max.6, f32[3072]{0:T(1024)S(1)} %multiply_add_fusion, f32[1536]{0:T(1024)S(1)} %get-tuple-element.32, f32[]{:T(128)S(6)} %mul.84), kind=kLoop, calls=%fused_computation.5 | loop fusion | flops 28311552 | bytes 47204360 | tf_op jit(solution)/shard_map/sub | solution.py:49
  158.5 76.3 %all-gather.2.cloned.1.call-done = bf16[6144,768]{1,0:T(8,128)(2,1)} async-done(((bf16[1536,768]{1,0:T(8,128)(2,1)}), bf16[6144,768]{1,0:T(8,128)(2,1)}) %all-gather.2.cloned.1.call-update) | async-done | bytes 9437200 | tf_op jit(solution)/shard_map/all_gather | solution.py:51
  234.8 8.0 %copy.16 = bf16[6144,768]{1,0:T(8,128)(2,1)} copy(bf16[6144,768]{1,0:T(8,128)(2,1)} %all-gather.2.cloned.1.call-done) | data formatting | bytes 18874368
  (17 shorter events, 0.0 us)
Async XLA Ops:
  7.2 12.0 %copy-start = (bf16[1536,768]{1,0:T(8,128)(2,1)S(1)}, bf16[1536,768]{1,0:T(8,128)(2,1)}, u32[]{:S(2)}) copy-start(bf16[1536,768]{1,0:T(8,128)(2,1)} %param.13) | copy-start | bytes 7077892
  7.2 227.6 %all-gather.2.cloned.1.call-start = ((), (), s32[]{:S(2)}) async-start(), calls=%async_computation | async-start | bytes 11796480 | tf_op jit(solution)/shard_map/all_gather | solution.py:51
  19.2 60.4 %copy-start.5 = (f32[3072]{0:T(1024)S(1)}, f32[3072]{0:T(1024)}, u32[]{:S(2)}) copy-start(f32[3072]{0:T(1024)} %param.11) | copy-start | bytes 36868
  19.2 60.4 %copy-start.6 = (f32[1536]{0:T(1024)S(1)}, f32[1536]{0:T(1024)}, u32[]{:S(2)}) copy-start(f32[1536]{0:T(1024)} %param.14) | copy-start | bytes 18436
  19.2 60.4 %copy-start.7 = (f32[1536]{0:T(1024)S(1)}, f32[1536]{0:T(1024)}, u32[]{:S(2)}) copy-start(f32[1536]{0:T(1024)} %param.10) | copy-start | bytes 18436
  20.2 69.0 %copy-start.8 = (f32[768]{0:T(1024)S(1)}, f32[768]{0:T(1024)}, u32[]{:S(2)}) copy-start(f32[768]{0:T(1024)} %param.15) | copy-start | bytes 9220
  20.2 71.5 %slice-start = ((s8[4718592]{0:T(1024)(128)(4,1)}), s8[524288]{0:T(1024)(128)(4,1)S(1)}, s32[]{:S(2)}) async-start(s8[4718592]{0:T(1024)(128)(4,1)} %bitcast), calls=%async_computation.1 | async-start | bytes 1048576
  79.6 59.5 %copy-start.1 = (f32[3072]{0:T(1024)}, f32[3072]{0:T(1024)S(1)}, u32[]{:S(2)}) copy-start(f32[3072]{0:T(1024)S(1)} %multiply_add_fusion) | copy-start | bytes 36868
  79.6 58.1 %copy-start.2 = (f32[1536]{0:T(1024)}, f32[1536]{0:T(1024)S(1)}, u32[]{:S(2)}) copy-start(f32[1536]{0:T(1024)S(1)} %get-tuple-element.34) | copy-start | bytes 18436
  79.6 59.5 %copy-start.3 = (f32[1536]{0:T(1024)}, f32[1536]{0:T(1024)S(1)}, u32[]{:S(2)}) copy-start(f32[1536]{0:T(1024)S(1)} %get-tuple-element.32) | copy-start | bytes 18436
  79.7 12.1 %slice-start.1 = ((s8[4718592]{0:T(1024)(128)(4,1)}), s8[4194304]{0:T(1024)(128)(4,1)S(1)}, s32[]{:S(2)}) async-start(s8[4718592]{0:T(1024)(128)(4,1)} %bitcast), calls=%async_computation.2 | async-start | bytes 8388608
  89.2 48.5 %copy-start.4 = (f32[768]{0:T(1024)}, f32[768]{0:T(1024)S(1)}, u32[]{:S(2)}) copy-start(f32[768]{0:T(1024)S(1)} %multiply_add_fusion.3) | copy-start | bytes 9220
Sparse Core Ops, SparseCore 0:
  137.8 96.8 all-gather.1
where the time goes:
time: 250 us
  blocking collectives  83.6 us (33%)
  waiting for transfers between devices  76.3 us (31%)
  other arithmetic  64.7 us (26%)
  between operations  17 us (7%)
  local copies, waits for them, and re-layouts  8.09 us (3%)
    all_gather x1, waiting for transfers between devices, local(): lax.all_gather(attn_new.astype(jnp.bfloat16), 'row', axis=0, tiled=True)  76.3 us
    psum x1, blocking collectives, local(): lax.psum((clip_local[0], clip_local[1]), ('row', 'col'))  37.2 us
    psum x1, blocking collectives, local(): lax.psum((jnp.sum(mlp_square, axis=1), jnp.sum(attn_square, axis=1)), 'col')  30.3 us
    sub x1, other arithmetic, local(): mlp_new = mlp_param - mlp_step * (mlp_raw / mlp_clip)  19.4 us
    psum x1, blocking collectives, local(): lax.psum((jnp.sum(mlp_square, axis=0), jnp.sum(attn_square, axis=0)), 'row')  16 us
    reduce_sum x1, other arithmetic, local(): jnp.sum(mlp_square, axis=1)  13 us
    reduce_sum x2, other arithmetic, local(): clip_local = (jnp.sum(jnp.square(mlp_raw)), jnp.sum(jnp.square(attn_raw)))  12.1 us
    reduce_sum x1, other arithmetic, local(): jnp.sum(jnp.square(mlp_param))  12 us
  transfers between devices with their start and end apart: 1, of which 1 were waited for; matrix products, arithmetic and copies ran while one was open for 8% of the time, Pallas kernels for 0%

commit v1 on v0

--- a/solution.py
+++ b/solution.py
@@ -1,12 +1,22 @@
+import functools
 import jax
 import jax.numpy as jnp
 from jax import lax
 from jax.sharding import PartitionSpec as P
+from jax.lax import psum
 
 STEP = 4
 TINY_SQUARE = 1e-30
 LEARN_RATE = 0.05
 DECAY_POWER = 0.8
+
+
+def mix_task(array_in, shard_axis, peer_axis):
+    y2 = psum(psum(array_in, shard_axis), peer_axis)
+    return y2
+
+
+turns_edit = functools.partial(mix_task, shard_axis="col", peer_axis="row")
 
 
 def local(
@@ -41,7 +51,7 @@
         attn_rows_new[:, None] * attn_cols_new[None, :]
     )
     clip_local = (jnp.sum(jnp.square(mlp_raw)), jnp.sum(jnp.square(attn_raw)))
-    clip_mlp, clip_attn = lax.psum((clip_local[0], clip_local[1]), ("row", "col"))
+    clip_mlp, clip_attn = turns_edit((clip_local[0], clip_local[1]))
     mlp_clip = jnp.maximum(1.0, jnp.sqrt(clip_mlp / mlp_count))
     attn_clip = jnp.maximum(1.0, jnp.sqrt(clip_attn / attn_count))
     mlp_step = LEARN_RATE * jnp.sqrt(param_mlp / mlp_count)

time: 250 us -> 273 us (1.092)
  blocking collectives: 83.6 us -> 107 us
  waiting for transfers between devices: 76.3 us -> 73.2 us
    psum x1 -> x3, blocking collectives: 37.2 us -> 64.8 us  [the longest x1 42.5 us: local(): lax.psum((param_local[0], param_local[1]), ('row', 'col'))]
    psum x1, blocking collectives: 30.3 us -> 26.8 us  [local(): lax.psum((jnp.sum(mlp_square, axis=1), jnp.sum(attn_square, axis=1)), 'col')]
    all_gather x1, waiting for transfers between devices: 76.3 us -> 73.1 us  [local(): lax.all_gather(attn_new.astype(jnp.bfloat16), 'row', axis=0, tiled=True)]
    unnamed x23 -> x19, local copies, waits for them, and re-layouts: 8.09 us -> 8.07 us
  transfers between devices with their start and end apart: 1 -> 1, of which waited for: 1 -> 1; matrix products, arithmetic and copies ran while one was open for 8% -> 7% of each run, Pallas kernels for 0% -> 0%
where the time goes in v1:
time: 273 us
  blocking collectives  107 us (39%)
  waiting for transfers between devices  73.2 us (27%)
  other arithmetic  67 us (25%)
  between operations  16.9 us (6%)
  local copies, waits for them, and re-layouts  8.07 us (3%)
    all_gather x1, waiting for transfers between devices, local(): lax.all_gather(attn_new.astype(jnp.bfloat16), 'row', axis=0, tiled=True)  73.1 us
    psum x1, blocking collectives, local(): lax.psum((param_local[0], param_local[1]), ('row', 'col'))  42.5 us
    psum x1, blocking collectives, local(): lax.psum((jnp.sum(mlp_square, axis=1), jnp.sum(attn_square, axis=1)), 'col')  26.8 us
    psum x2, blocking collectives, mix_task(): y2 = psum(psum(array_in, shard_axis), peer_axis)  22.3 us
    sub x1, other arithmetic, local(): mlp_new = mlp_param - mlp_step * (mlp_raw / mlp_clip)  19.6 us
    psum x1, blocking collectives, local(): lax.psum((jnp.sum(mlp_square, axis=0), jnp.sum(attn_square, axis=0)), 'row')  15.9 us
    reduce_sum x1, other arithmetic, local(): jnp.sum(mlp_square, axis=1)  13.1 us
    reduce_sum x2, other arithmetic, local(): clip_local = (jnp.sum(jnp.square(mlp_raw)), jnp.sum(jnp.square(attn_raw)))  11.9 us
  transfers between devices with their start and end apart: 1, of which 1 were waited for; matrix products, arithmetic and copies ran while one was open for 7% of the time, Pallas kernels for 0%

profile of v1, /device:TPU:0, one launch (start us, length us, event | category | flops | bytes accessed | tf_op | source)
XLA Modules:
  0.0 272.6 jit_solution(15233676696966110958)
XLA Ops:
  7.2 0.0 all-gather.2.cloned.1.call-start
  7.2 4.2 %multiply_reduce_fusion.3 = f32[]{:T(128)} fusion(f32[1536,768]{1,0:T(8,128)} %param.12), kind=kLoop, calls=%fused_computation.15 | loop fusion | flops 2359295 | bytes 4718596 | tf_op jit(solution)/shard_map/reduce_sum | solution.py:41
  11.4 11.8 %multiply_reduce_fusion.1 = f32[]{:T(128)} fusion(f32[1536,3072]{1,0:T(8,128)} %param.8), kind=kLoop, calls=%fused_computation.7 | loop fusion | flops 9437183 | bytes 18874372 | tf_op jit(solution)/shard_map/reduce_sum | solution.py:41
  23.2 13.1 %fusion.2 = (f32[1536]{0:T(1024)S(1)}, f32[3072]{0:T(1024)S(1)}) fusion(bf16[1536,3072]{1,0:T(8,128)(2,1)} %param.9), kind=kLoop, calls=%fused_computation.4 | loop fusion | flops 23588352 | bytes 9455616 | tf_op jit(solution)/shard_map/reduce_sum | solution.py:43
  36.3 0.0 copy-done
  36.3 1.0 fusion.5
  37.3 42.5 %all-reduce = (f32[]{:T(128)}, f32[]{:T(128)}) all-reduce(f32[]{:T(128)} %multiply_reduce_fusion.1, f32[]{:T(128)} %multiply_reduce_fusion.3), channel_id=1, replica_groups=mesh['row'=4,'col'=8] {'row','col'}, use_global_device_ids=true, to_apply=%region_1.0 | all-reduce | flops 2 | bytes 16 | tf_op jit(solution)/shard_map/psum | solution.py:42
  80.4 26.8 %all-reduce.2 = (f32[1536]{0:T(1024)S(1)}, f32[1536]{0:T(1024)S(1)}) all-reduce(f32[1536]{0:T(1024)S(1)} %get-tuple-element.7, f32[1536]{0:T(1024)S(1)} %get-tuple-element.9), channel_id=1, replica_groups=mesh['row'=4,'col'=8] {'col'}, use_global_device_ids=true, to_apply=%region_3.0 | all-reduce | flops 3072 | bytes 24576 | tf_op jit(solution)/shard_map/psum | solution.py:43
  107.3 15.9 %all-reduce.4 = (f32[3072]{0:T(1024)S(1)}, f32[768]{0:T(1024)S(1)}) all-reduce(f32[3072]{0:T(1024)S(1)} %get-tuple-element.8, f32[768]{0:T(1024)S(1)} %get-tuple-element.10), channel_id=1, replica_groups=mesh['row'=4,'col'=8] {'row'}, use_global_device_ids=true, to_apply=%region_5.0 | all-reduce | flops 3840 | bytes 30720 | tf_op jit(solution)/shard_map/psum | solution.py:46
  123.1 0.0 copy-done.5
  123.1 0.0 copy-start.1
  123.2 0.0 copy-done.6
  123.2 0.0 copy-start.2
  123.2 0.0 copy-start.3
  123.2 9.4 %multiply_reduce_fusion = f32[]{:T(128)} fusion(bf16[1536,3072]{1,0:T(8,128)(2,1)} %param.9, f32[3072]{0:T(1024)S(1)} %multiply_add_fusion, f32[1536]{0:T(1024)S(1)} %get-tuple-element.34), kind=kLoop, calls=%fused_computation.6 | loop fusion | flops 23592960 | bytes 9455620 | tf_op jit(solution)/shard_map/reduce_sum | solution.py:53
  132.6 2.5 multiply_reduce_fusion.2
  135.2 14.2 %all-reduce.1 = (f32[]{:T(128)}, f32[]{:T(128)}) all-reduce(f32[]{:T(128)} %multiply_reduce_fusion, f32[]{:T(128)} %multiply_reduce_fusion.2), channel_id=1, replica_groups=mesh['row'=4,'col'=8] {'col'}, use_global_device_ids=true, to_apply=%region_7.0 | all-reduce | flops 2 | bytes 16 | tf_op jit(solution)/shard_map/psum | solution.py:15
  149.4 8.1 %all-reduce.3 = (f32[]{:T(128)}, f32[]{:T(128)}) all-reduce(f32[]{:T(128)} %get-tuple-element.13, f32[]{:T(128)} %get-tuple-element.14), channel_id=1, replica_groups=mesh['row'=4,'col'=8] {'row'}, use_global_device_ids=true, to_apply=%region_8.0 | all-reduce | flops 2 | bytes 16 | tf_op jit(solution)/shard_map/psum | solution.py:15
  158.2 5.4 %fusion.6 = (bf16[1536,768]{1,0:T(8,128)(2,1)}, f32[1536,768]{1,0:T(8,128)}) fusion(f32[1536,768]{1,0:T(8,128)} %param.12, f32[]{:T(128)S(6)} %max.7, f32[768]{0:T(1024)S(1)} %multiply_add_fusion.3, f32[1536]{0:T(1024)S(1)} %get-tuple-element.36, bf16[1536,768]{1,0:T(8,128)(2,1)S(1)} %copy-done, f32[]{:T(128)S(6)} %mul.97), kind=kLoop, calls=%fused_computation.20 | loop fusion | flops 8257536 | bytes 14165000 | tf_op jit(solution)/shard_map/convert_element_type | solution.py:61
  163.6 0.0 all-gather.2.cloned.1.call-update
  163.6 0.0 copy-done.4
  165.0 19.6 %multiply_subtract_fusion = f32[1536,3072]{1,0:T(8,128)} fusion(f32[1536,3072]{1,0:T(8,128)} %param.8, bf16[1536,3072]{1,0:T(8,128)(2,1)} %param.9, f32[]{:T(128)S(6)} %max.6, f32[3072]{0:T(1024)S(1)} %multiply_add_fusion, f32[1536]{0:T(1024)S(1)} %get-tuple-element.34, f32[]{:T(128)S(6)} %mul.84), kind=kLoop, calls=%fused_computation.5 | loop fusion | flops 28311552 | bytes 47204360 | tf_op jit(solution)/shard_map/sub | solution.py:59
  184.6 73.1 %all-gather.2.cloned.1.call-done = bf16[6144,768]{1,0:T(8,128)(2,1)} async-done(((bf16[1536,768]{1,0:T(8,128)(2,1)}), bf16[6144,768]{1,0:T(8,128)(2,1)}) %all-gather.2.cloned.1.call-update) | async-done | bytes 9437200 | tf_op jit(solution)/shard_map/all_gather | solution.py:61
  257.8 8.0 %copy.16 = bf16[6144,768]{1,0:T(8,128)(2,1)} copy(bf16[6144,768]{1,0:T(8,128)(2,1)} %all-gather.2.cloned.1.call-done) | data formatting | bytes 18874368
  (14 shorter events, 0.0 us)
Async XLA Ops:
  7.2 250.6 %all-gather.2.cloned.1.call-start = ((), (), s32[]{:S(2)}) async-start(), calls=%async_computation | async-start | bytes 11796480 | tf_op jit(solution)/shard_map/all_gather | solution.py:61
  23.2 13.1 %copy-start = (bf16[1536,768]{1,0:T(8,128)(2,1)S(1)}, bf16[1536,768]{1,0:T(8,128)(2,1)}, u32[]{:S(2)}) copy-start(bf16[1536,768]{1,0:T(8,128)(2,1)} %param.13) | copy-start | bytes 7077892
  23.2 99.9 %copy-start.5 = (f32[3072]{0:T(1024)S(1)}, f32[3072]{0:T(1024)}, u32[]{:S(2)}) copy-start(f32[3072]{0:T(1024)} %param.11) | copy-start | bytes 36868
  23.2 100.0 %copy-start.6 = (f32[1536]{0:T(1024)S(1)}, f32[1536]{0:T(1024)}, u32[]{:S(2)}) copy-start(f32[1536]{0:T(1024)} %param.14) | copy-start | bytes 18436
  23.2 100.0 %copy-start.7 = (f32[1536]{0:T(1024)S(1)}, f32[1536]{0:T(1024)}, u32[]{:S(2)}) copy-start(f32[1536]{0:T(1024)} %param.10) | copy-start | bytes 18436
  23.2 109.4 %copy-start.8 = (f32[768]{0:T(1024)S(1)}, f32[768]{0:T(1024)}, u32[]{:S(2)}) copy-start(f32[768]{0:T(1024)} %param.15) | copy-start | bytes 9220
  123.1 41.8 %copy-start.1 = (f32[3072]{0:T(1024)}, f32[3072]{0:T(1024)S(1)}, u32[]{:S(2)}) copy-start(f32[3072]{0:T(1024)S(1)} %multiply_add_fusion) | copy-start | bytes 36868
  123.2 40.4 %copy-start.2 = (f32[1536]{0:T(1024)}, f32[1536]{0:T(1024)S(1)}, u32[]{:S(2)}) copy-start(f32[1536]{0:T(1024)S(1)} %get-tuple-element.36) | copy-start | bytes 18436
  123.2 41.8 %copy-start.3 = (f32[1536]{0:T(1024)}, f32[1536]{0:T(1024)S(1)}, u32[]{:S(2)}) copy-start(f32[1536]{0:T(1024)S(1)} %get-tuple-element.34) | copy-start | bytes 18436
  132.6 31.0 %copy-start.4 = (f32[768]{0:T(1024)}, f32[768]{0:T(1024)S(1)}, u32[]{:S(2)}) copy-start(f32[768]{0:T(1024)S(1)} %multiply_add_fusion.3) | copy-start | bytes 9220
Sparse Core Ops, SparseCore 0:
  163.7 93.9 all-gather.1
